TPU v7x, 32 devices: a whole 2x2x4 slice. The times are simulated.
32 devices in a mesh: tp: 8 (over y, x, core), col: 4 (over z).
Axes of the slice: x: 2, y: 2, z: 4, core: 2. Of those that a mesh axis runs over, the one named last changes fastest.
Arguments:
- gate_in: bfloat16 [128, 53248], P('col', 'tp'), may hold values from -6 to 6
- up_in: bfloat16 [128, 53248], P('col', 'tp'), may hold values from -6 to 6
- down_weight: bfloat16 [53248, 16384], P('tp', 'col'), may hold values from -0.02734375 to 0.02734375
- residual: bfloat16 [128, 16384], P('tp', 'col'), may hold values from -30 to 30
- norm_gain: bfloat16 [16384], P('col'), may hold values from 0.5 to 1.5
Outputs:
- stream: bfloat16 [128, 16384], P('tp', 'col')
- normed: bfloat16 [128, 16384], P('tp', 'col')
All inputs are finite; a program needn't handle non-finite values.
Results may differ from a plain program's by a relative error of at most 0.0034.
Values may be sent and summed in bfloat16 or wider, within the bound.
A program may use at most 128 MiB of HBM per device.

v0:
```python
import jax
import jax.numpy as jnp
from jax import lax
from jax.sharding import PartitionSpec as P

D = 16384


def gated(gate_part, up_part):
    return (jax.nn.silu(gate_part.astype(jnp.float32)) * up_part.astype(jnp.float32)).astype(
        jnp.bfloat16
    )


def body(gate_in, up_in, down_weight, residual, norm_gain):
    local_act = gated(gate_in, up_in)
    hidden = lax.all_gather(local_act, "col", axis=0, tiled=True)
    partial_value = jnp.dot(hidden, down_weight, preferred_element_type=jnp.float32)
    branch = lax.psum_scatter(partial_value, "tp", scatter_dimension=0, tiled=True)
    summed = residual.astype(jnp.float32) + branch
    local_squares = jnp.sum(summed * summed, axis=1, keepdims=True)
    mean_square = lax.psum(local_squares, "col") / D
    scaled = summed * lax.rsqrt(mean_square + 1e-05) * norm_gain.astype(jnp.float32)[None, :]
    return (summed.astype(jnp.bfloat16), scaled.astype(jnp.bfloat16))


def solution(mesh):
    in_specs = (P("col", "tp"), P("col", "tp"), P("tp", "col"), P("tp", "col"), P("col"))
    out_specs = (P("tp", "col"), P("tp", "col"))
    return jax.shard_map(body, mesh=mesh, in_specs=in_specs, out_specs=out_specs, check_vma=False)
```

profile of v0, /device:TPU:0, one launch (start us, length us, event | category | flops | bytes accessed | tf_op | source)
XLA Modules:
  0.0 134.5 jit_solution(9100638335402482563)
XLA Ops:
  7.2 0.0 all-gather.2.cloned.1.call-start
  7.2 2.1 %fusion.4 = bf16[32,6656]{1,0:T(8,128)(2,1)} fusion(bf16[32,6656]{1,0:T(8,128)(2,1)} %param.6, bf16[32,6656]{1,0:T(8,128)(2,1)} %param.5), kind=kLoop, calls=%fused_computation.6 | loop fusion | flops 1703936 | bytes 1277952 | tf_op jit(solution)/shard_map/convert_element_type | solution.py:10
  9.4 0.0 all-gather.2.cloned.1.call-update
  9.4 0.0 reduce-scatter.2.cloned.1.call-start
  9.4 42.0 %all-gather.2.cloned.1.call-done = bf16[128,6656]{1,0:T(8,128)(2,1)} async-done(((bf16[32,6656]{1,0:T(8,128)(2,1)}), bf16[128,6656]{1,0:T(8,128)(2,1)}) %all-gather.2.cloned.1.call-update) | async-done | bytes 1703952 | tf_op jit(solution)/shard_map/all_gather | solution.py:17
  51.5 21.5 %fusion.6 = f32[128,4096]{1,0:T(8,128)} fusion(bf16[128,6656]{1,0:T(8,128)(2,1)} %all-gather.2.cloned.1.call-done, bf16[6656,4096]{1,0:T(8,128)(2,1)} %param.7), kind=kOutput, calls=%fused_computation.12 | convolution fusion | flops 6979321856 | bytes 58327040 | tf_op jit(solution)/shard_map/dot_general | solution.py:18
  73.0 0.0 copy-start.1
  73.0 0.0 copy-start
  73.0 0.0 reduce-scatter.2.cloned.1.call-update
  73.0 0.7 copy-done.1
  73.7 39.4 %reduce-scatter.2.cloned.1.call-done = f32[16,4096]{1,0:T(8,128)} async-done(((f32[128,4096]{1,0:T(8,128)}), f32[16,4096]{1,0:T(8,128)}) %reduce-scatter.2.cloned.1.call-update) | async-done | bytes 262160 | tf_op jit(solution)/shard_map/reduce_scatter | solution.py:19
  113.1 0.0 copy-done
  113.1 1.1 multiply_reduce_fusion
  114.2 11.7 %psum.7 = f32[16,1]{0,1:T(1,128)S(1)} all-reduce(f32[16,1]{0,1:T(1,128)S(1)} %bitcast.5), channel_id=1, replica_groups=mesh['tp'=8,'col'=4] {'col'}, use_global_device_ids=true, to_apply=%region_2.3 | all-reduce | flops 16 | bytes 128 | tf_op jit(solution)/shard_map/psum | solution.py:22
  125.9 1.7 %multiply_convert_fusion = (bf16[16,4096]{1,0:T(8,128)(2,1)}, bf16[16,4096]{1,0:T(8,128)(2,1)}) fusion(f32[4096]{0:T(1024)S(1)} %convert_element_type.26, f32[16]{0:T(128)S(1)} %rsqrt_bitcast_fusion, f32[16,4096]{1,0:T(8,128)} %reduce-scatter.2.cloned.1.call-done, bf16[16,4096]{1,0:T(8,128)(2,1)S(1)} %copy-done), kind=kLoop, calls=%fused_computation.7 | loop fusion | flops 393216 | bytes 671808 | tf_op jit(solution)/shard_map/convert_element_type | solution.py:24
  (2 shorter events, 0.0 us)
Async XLA Ops:
  7.2 44.3 %all-gather.2.cloned.1.call-start = ((), (), s32[]{:S(2)}) async-start(), calls=%async_computation.1 | async-start | bytes 2129920 | tf_op jit(solution)/shard_map/all_gather | solution.py:17
  9.4 103.7 %reduce-scatter.2.cloned.1.call-start = ((), (), s32[]{:S(2)}) async-start(), calls=%async_computation.2 | async-start | bytes 2359296 | tf_op jit(solution)/shard_map/reduce_scatter | solution.py:19
  73.0 0.7 copy-start.1
  73.0 40.1 %copy-start = (bf16[16,4096]{1,0:T(8,128)(2,1)S(1)}, bf16[16,4096]{1,0:T(8,128)(2,1)}, u32[]{:S(2)}) copy-start(bf16[16,4096]{1,0:T(8,128)(2,1)} %param.8) | copy-start | bytes 393220
Sparse Core Ops, SparseCore 0:
  9.5 41.8 all-gather.1
  73.1 39.9 reduce-scatter.1
where the time goes:
time: 135 us; the launch traced here: 134 us
  waiting for transfers between devices  81.5 us (60%)
  matrix products  21.5 us (16%)
  between operations  14 us (10%)
  blocking collectives  11.7 us (9%)
  other arithmetic  4.96 us (4%)
    all_gather x1, waiting for transfers between devices, body(): hidden = lax.all_gather(local_act, 'col', axis=0, tiled=True)  42 us
    reduce_scatter x1, waiting for transfers between devices, body(): lax.psum_scatter(partial_value, 'tp', scatter_dimension=0, tiled=True)  39.4 us
    dot_general x1, matrix products, body(): jnp.dot(hidden, down_weight, preferred_element_type=jnp.float32)  21.5 us
    psum x1, blocking collectives, body(): mean_square = lax.psum(local_squares, 'col') / D  11.7 us
  transfers between devices with their start and end apart: 2, of which 2 were waited for; matrix products, arithmetic and copies ran while one was open for 0% of the time, Pallas kernels for 0%

commit v1 on v0

v1 whole, which is shorter than its diff:
```python
import functools

import jax
import jax.numpy as jnp
from jax import lax
from jax.experimental import pallas as pl
from jax.experimental.pallas import tpu as pltpu
from jax.sharding import PartitionSpec as P

MESH = pl.DeviceIdType.MESH
VMEM_BYTES = 67_043_328
EPS = 1e-05


def gated(gate_part, up_part):
    return (jax.nn.silu(gate_part.astype(jnp.float32)) * up_part.astype(jnp.float32)).astype(
        jnp.bfloat16
    )


def plain_body(width, gate_in, up_in, down_weight, residual, norm_gain):
    local_act = gated(gate_in, up_in)
    hidden = lax.all_gather(local_act, "col", axis=0, tiled=True)
    partial_value = jnp.dot(hidden, down_weight, preferred_element_type=jnp.float32)
    branch = lax.psum_scatter(partial_value, "tp", scatter_dimension=0, tiled=True)
    summed = residual.astype(jnp.float32) + branch
    local_squares = jnp.sum(summed * summed, axis=1, keepdims=True)
    mean_square = lax.psum(local_squares, "col") / width
    scaled = summed * lax.rsqrt(mean_square + EPS) * norm_gain.astype(jnp.float32)[None, :]
    return (summed.astype(jnp.bfloat16), scaled.astype(jnp.bfloat16))


def pick(extent, most, step):
    best = 0
    for size in range(step, min(extent, most) + 1, step):
        if extent % size == 0:
            best = size
    return best


def kernel(
    n_col, n_pair, kp, nt, rt, skew,
    gate_hbm, up_hbm, w_hbm, res_hbm,
    out_hbm, sq_out,
    gate_v, up_v, hid, w_v, acc, peer, send_buf, recv_buf, own, res_v, total, squares,
    in_sem, w_sem, res_sem, out_sem, ag_send, ag_recv, d_send, d_recv, r_send, r_recv, q_send, q_recv,
):
    rows, depth = gate_hbm.shape
    width = w_hbm.shape[1]
    pieces = depth // kp
    tiles = width // rt
    me = lax.axis_index("tp")
    z = lax.axis_index("col")
    plane, core = me // 2, lax.rem(me, 2)

    barrier = pltpu.get_barrier_semaphore()
    for step in range(1, n_col):
        pl.semaphore_signal(
            barrier, inc=1, device_id={"col": lax.rem(z + step, n_col)}, device_id_type=MESH
        )
    pl.semaphore_signal(barrier, inc=1, device_id={"tp": 2 * plane + 1 - core}, device_id_type=MESH)
    for step in range(1, n_pair):
        pl.semaphore_signal(
            barrier,
            inc=1,
            device_id={"tp": 2 * lax.rem(plane + step, n_pair) + core},
            device_id_type=MESH,
        )

    def cols(s):
        return pl.ds(pl.multiple_of(s * kp, kp), kp)

    def load(s, which):
        src, dst = ((gate_hbm, gate_v), (up_hbm, up_v))[which]
        return pltpu.make_async_copy(src.at[:, cols(s)], dst.at[:, cols(s)], in_sem.at[which, s])

    def load_w(s):
        return pltpu.make_async_copy(w_hbm.at[cols(s), :], w_v.at[cols(s), :], w_sem.at[s])

    load_res = pltpu.make_async_copy(res_hbm, res_v, res_sem)

    @pl.loop(0, pieces)
    def _(s):
        load(s, 0).start()
        load(s, 1).start()

    @pl.loop(0, pieces)
    def _(s):
        load_w(s).start()

    load_res.start()

    def hid_rows(source):
        return pl.ds(pl.multiple_of(source * rows, rows), rows)

    def hop(source, s, up):
        block = hid.at[hid_rows(source), cols(s)]
        return pltpu.make_async_remote_copy(
            src_ref=block,
            dst_ref=block,
            send_sem=ag_send.at[0 if up else 1, source],
            recv_sem=ag_recv.at[source, s],
            device_id={"col": z + 1 if up else z - 1},
            device_id_type=MESH,
        )

    def send_both(source, s):
        @pl.when(z < n_col - 1)
        def _():
            hop(source, s, True).start()

        @pl.when(z > 0)
        def _():
            hop(source, s, False).start()

    pl.semaphore_wait(barrier, n_col - 1 + 1 + n_pair - 1)

    @pl.loop(0, pieces + 1)
    def _(s):
        @pl.when(s < pieces)
        def _():
            load(s, 0).wait()
            load(s, 1).wait()
            g = gate_v[:, cols(s)].astype(jnp.float32)
            u = up_v[:, cols(s)].astype(jnp.float32)
            hid[hid_rows(z), cols(s)] = (g / (1.0 + jnp.exp(-g)) * u).astype(jnp.bfloat16)

        @pl.when(s > 0)
        def _():
            send_both(z, s - 1)

    acc[...] = jnp.zeros_like(acc)

    @pl.loop(0, pieces + skew * (n_col - 2))
    def _(i):
        for away in range(n_col - 1, 0, -1):
            s = i - skew * (away - 1)
            live = jnp.logical_and(s >= 0, s < pieces)

            @pl.when(jnp.logical_and(live, z - away >= 0))
            def _():
                hop(z - away, s, True).wait_recv()

                @pl.when(z < n_col - 1)
                def _():
                    hop(z - away, s, True).start()

            @pl.when(jnp.logical_and(live, z + away < n_col))
            def _():
                hop(z + away, s, False).wait_recv()

                @pl.when(z > 0)
                def _():
                    hop(z + away, s, False).start()

        s = i - skew * (n_col - 2)

        @pl.when(s >= 0)
        def _():
            load_w(s).wait()
            a = hid[:, cols(s)]
            for n in range(width // nt):
                part = jnp.dot(
                    a, w_v[cols(s), n * nt : (n + 1) * nt], preferred_element_type=jnp.float32
                )
                acc[:, :, :, n * nt : (n + 1) * nt] += part.reshape(acc.shape[:3] + (nt,))

    def swap(n):
        return pltpu.make_async_remote_copy(
            src_ref=acc.at[:, 1 - core, :, n * rt : (n + 1) * rt],
            dst_ref=peer.at[:, :, n * rt : (n + 1) * rt],
            send_sem=d_send,
            recv_sem=d_recv.at[n],
            device_id={"tp": 2 * plane + 1 - core},
            device_id_type=MESH,
        )

    def scatter(n, step):
        to = lax.rem(plane + step, n_pair)
        return pltpu.make_async_remote_copy(
            src_ref=send_buf.at[to, :, n * rt : (n + 1) * rt],
            dst_ref=recv_buf.at[step - 1, :, n * rt : (n + 1) * rt],
            send_sem=r_send.at[step - 1],
            recv_sem=r_recv.at[step - 1, n],
            device_id={"tp": 2 * to + core},
            device_id_type=MESH,
        )

    for n in range(tiles):
        swap(n).start()
    load_res.wait()
    for n in range(tiles + 1):
        if n < tiles:
            here = slice(n * rt, (n + 1) * rt)
            swap(n).wait_recv()
            both = acc[:, core, :, here] + peer[:, :, here]
            send_buf[:, :, here] = both.astype(jnp.bfloat16)
            own[:, here] = (
                acc[plane, core, :, here] + peer[plane, :, here]
                + res_v[:, here].astype(jnp.float32)
            )
        if n > 0:
            for step in range(1, n_pair):
                scatter(n - 1, step).start()

    sums = jnp.zeros((res_hbm.shape[0], 128), jnp.float32)
    writes = []
    for n in range(tiles):
        here = slice(n * rt, (n + 1) * rt)
        value = own[:, here]
        for step in range(1, n_pair):
            scatter(n, step).wait_recv()
            value = value + recv_buf[step - 1, :, here].astype(jnp.float32)
        total[:, here] = value
        square = value * value
        for j in range(rt // 128):
            sums = sums + square[:, j * 128 : (j + 1) * 128]
        write = pltpu.make_async_copy(total.at[:, here], out_hbm.at[:, here], out_sem.at[n])
        write.start()
        writes.append(write)

    squares[z] = jnp.broadcast_to(jnp.sum(sums, axis=1, keepdims=True), sums.shape)

    def share(step):
        return pltpu.make_async_remote_copy(
            src_ref=squares.at[z],
            dst_ref=squares.at[z],
            send_sem=q_send.at[step - 1],
            recv_sem=q_recv.at[step - 1],
            device_id={"col": lax.rem(z + step, n_col)},
            device_id_type=MESH,
        )

    def arrival(step):
        block = squares.at[lax.rem(z + n_col - step, n_col)]
        return pltpu.make_async_remote_copy(
            src_ref=block,
            dst_ref=block,
            send_sem=q_send.at[step - 1],
            recv_sem=q_recv.at[step - 1],
            device_id={"col": lax.rem(z + step, n_col)},
            device_id_type=MESH,
        )

    for step in range(1, n_col):
        share(step).start()

    for source in range(n_col):
        block = hid.at[source * rows : (source + 1) * rows, :]
        for up in (0, 1):
            sent = jnp.logical_and(source <= z, z < n_col - 1)
            if not up:
                sent = jnp.logical_and(source >= z, z > 0)

            @pl.when(sent)
            def _():
                pltpu.make_async_remote_copy(
                    src_ref=block,
                    dst_ref=block,
                    send_sem=ag_send.at[0 if up else 1, source],
                    recv_sem=ag_recv.at[source, 0],
                    device_id={"col": z + 1 if up else z - 1},
                    device_id_type=MESH,
                ).wait_send()

    pltpu.make_async_remote_copy(
        src_ref=peer,
        dst_ref=peer,
        send_sem=d_send,
        recv_sem=d_recv.at[0],
        device_id={"tp": 2 * plane + 1 - core},
        device_id_type=MESH,
    ).wait_send()
    for step in range(1, n_pair):
        to = lax.rem(plane + step, n_pair)
        pltpu.make_async_remote_copy(
            src_ref=send_buf.at[to],
            dst_ref=recv_buf.at[step - 1],
            send_sem=r_send.at[step - 1],
            recv_sem=r_recv.at[step - 1, 0],
            device_id={"tp": 2 * to + core},
            device_id_type=MESH,
        ).wait_send()
    for write in writes:
        write.wait()
    for step in range(1, n_col):
        share(step).wait_send()
        arrival(step).wait_recv()
    whole = squares[0]
    for j in range(1, n_col):
        whole = whole + squares[j]
    sq_out[...] = whole


def fused_body(n_tp, n_col, kp, nt, rt, width, gate_in, up_in, down_weight, residual, norm_gain):
    rows, depth = gate_in.shape
    local = down_weight.shape[1]
    own_rows = residual.shape[0]
    n_pair = n_tp // 2
    pieces, tiles = depth // kp, local // rt
    any_space = pl.BlockSpec(memory_space=pl.ANY)
    dma = pltpu.SemaphoreType.DMA
    summed, squares = pl.pallas_call(
        functools.partial(kernel, n_col, n_pair, kp, nt, rt, min(3, pieces)),
        out_shape=(
            jax.ShapeDtypeStruct((own_rows, local), jnp.float32),
            jax.ShapeDtypeStruct((own_rows, 128), jnp.float32),
        ),
        in_specs=[any_space] * 4,
        out_specs=(any_space, pl.BlockSpec(memory_space=pltpu.VMEM)),
        scratch_shapes=[
            pltpu.VMEM((rows, depth), jnp.bfloat16),
            pltpu.VMEM((rows, depth), jnp.bfloat16),
            pltpu.VMEM((rows * n_col, depth), jnp.bfloat16),
            pltpu.VMEM((depth, local), jnp.bfloat16),
            pltpu.VMEM((n_pair, 2, own_rows, local), jnp.float32),
            pltpu.VMEM((n_pair, own_rows, local), jnp.float32),
            pltpu.VMEM((n_pair, own_rows, local), jnp.bfloat16),
            pltpu.VMEM((n_pair - 1, own_rows, local), jnp.bfloat16),
            pltpu.VMEM((own_rows, local), jnp.float32),
            pltpu.VMEM((own_rows, local), jnp.bfloat16),
            pltpu.VMEM((own_rows, local), jnp.float32),
            pltpu.VMEM((n_col, own_rows, 128), jnp.float32),
            dma((2, pieces)),
            dma((pieces,)),
            dma,
            dma((tiles,)),
            dma((2, n_col)),
            dma((n_col, pieces)),
            dma,
            dma((tiles,)),
            dma((n_pair - 1,)),
            dma((n_pair - 1, tiles)),
            dma((n_col - 1,)),
            dma((n_col - 1,)),
        ],
        compiler_params=pltpu.CompilerParams(
            collective_id=0, has_side_effects=True, vmem_limit_bytes=VMEM_BYTES
        ),
        name="down_reduce",
    )(gate_in, up_in, down_weight, residual)
    mean_square = squares[:, :1] / width
    scaled = summed * lax.rsqrt(mean_square + EPS) * norm_gain.astype(jnp.float32)[None, :]
    return (summed.astype(jnp.bfloat16), scaled.astype(jnp.bfloat16))


def pairs_share_chip(mesh):
    if tuple(mesh.axis_names) != ("tp", "col") or mesh.shape["tp"] % 2 or mesh.shape["tp"] < 4:
        return False
    devices = mesh.devices
    for j in range(0, mesh.shape["tp"], 2):
        for a, b in zip(devices[j], devices[j + 1]):
            first = getattr(a, "coords", None)
            if first is None or list(first) != list(getattr(b, "coords", ())):
                return False
    return True


def solution(mesh):
    in_specs = (P("col", "tp"), P("col", "tp"), P("tp", "col"), P("tp", "col"), P("col"))
    out_specs = (P("tp", "col"), P("tp", "col"))
    n_tp, n_col = mesh.shape["tp"], mesh.shape["col"]

    def run(gate_in, up_in, down_weight, residual, norm_gain):
        tokens, hidden_units = gate_in.shape
        width = down_weight.shape[1]
        depth, local = hidden_units // n_tp, width // n_col
        rows, own_rows = tokens // n_col, tokens // n_tp
        kp, nt, rt = pick(depth, 512, 128), pick(local, 1024, 128), pick(local, 512, 128)
        need = 2 * depth * (local + tokens + 2 * rows) + local * tokens * 9 + (4 << 20)
        fused = (
            pairs_share_chip(mesh)
            and n_col > 1
            and rows % 16 == 0
            and own_rows % 16 == 0
            and kp > 0
            and nt > 0
            and need < VMEM_BYTES
        )
        body = functools.partial(plain_body, width)
        if fused:
            body = functools.partial(fused_body, n_tp, n_col, kp, nt, rt, width)
        return jax.shard_map(
            body, mesh=mesh, in_specs=in_specs, out_specs=out_specs, check_vma=False
        )(gate_in, up_in, down_weight, residual, norm_gain)

    return run
```

time: 135 us -> 54.2 us (0.40)
  waiting for transfers between devices: 81.5 us -> 0 us
  Pallas kernels: 0 us -> 49.5 us
  matrix products: 21.5 us -> 0 us
  between operations: 14 us -> 0.64 us
  blocking collectives: 11.7 us -> 0 us
    pallas_call x0 -> x1, Pallas kernels: none -> 49.5 us  [fused_body(): pl.pallas_call(functools.partial(kernel, n_col, n_pair, kp, nt, rt, min(3...]
    all_gather x1 -> x0, waiting for transfers between devices: 42 us -> none  [body(): hidden = lax.all_gather(local_act, 'col', axis=0, tiled=True)]
    reduce_scatter x1 -> x0, waiting for transfers between devices: 39.4 us -> none  [body(): lax.psum_scatter(partial_value, 'tp', scatter_dimension=0, tiled=True)]
    dot_general x1 -> x0, matrix products: 21.5 us -> none  [body(): jnp.dot(hidden, down_weight, preferred_element_type=jnp.float32)]
    psum x1 -> x0, blocking collectives: 11.7 us -> none  [body(): mean_square = lax.psum(local_squares, 'col') / D]
    convert_element_type x3 -> x2, other arithmetic: 3.85 us -> 3.08 us  [the longest x1 1.79 us: fused_body(): return (summed.astype(jnp.bfloat16), scaled.astype(jnp.bfloat16))]
  transfers between devices with their start and end apart: 2 -> 0, of which waited for: 2 -> 0; matrix products, arithmetic and copies ran while one was open for 0% -> 0% of each run, Pallas kernels for 0% -> 0%
where the time goes in v1:
time: 54.2 us; the launch traced here: 54 us
  Pallas kernels  49.5 us (91%)
  other arithmetic  3.9 us (7%)
  between operations  0.64 us (1%)
    pallas_call x1, Pallas kernels, fused_body(): pl.pallas_call(functools.partial(kernel, n_col, n_pair, kp, nt, rt, min(3...  49.5 us
    convert_element_type x1, other arithmetic, fused_body(): return (summed.astype(jnp.bfloat16), scaled.astype(jnp.bfloat16))  1.79 us
    convert_element_type x1, other arithmetic, fused_body(): norm_gain.astype(jnp.float32)[None, :]  1.3 us

profile of v1, /device:TPU:0, one launch (start us, length us, event | category | flops | bytes accessed | tf_op | source)
XLA Modules:
  0.0 54.0 jit_solution(18446219937844426578)
XLA Ops:
  0.6 1.3 %convert_element_type.10 = f32[4096]{0:T(1024)} convert(bf16[4096]{0:T(1024)(128)(2,1)} %param.9) | non-fusion elementwise | flops 4096 | bytes 24576 | tf_op jit(solution)/shard_map/convert_element_type | solution.py:343
  1.9 49.5 %down_reduce.1 = (f32[16,4096]{1,0:T(8,128)}, f32[16,128]{1,0:T(8,128)}) custom-call(bf16[32,6656]{1,0:T(8,128)(2,1)} %gate_hbm.1, bf16[32,6656]{1,0:T(8,128)(2,1)} %up_hbm.1, bf16[6656,4096]{1,0:T(8,128)(2,1)} %w_hbm.1, bf16[16,4096]{1,0:T(8,128)(2,1)} %res_hbm.1), custom_call_target="tpu_custom_call" | custom-call | tf_op jit(solution)/shard_map/down_reduce/pallas_call | solution.py:303
  51.4 0.8 %rsqrt_reduce_fusion = f32[16]{0:T(128)S(1)} fusion(f32[16,128]{1,0:T(8,128)} %get-tuple-element.5), kind=kLoop, calls=%fused_computation.1 | loop fusion | flops 32 | bytes 128 | tf_op jit(solution)/shard_map/rsqrt | solution.py:343
  52.2 1.8 %multiply_convert_fusion = (bf16[16,4096]{1,0:T(8,128)(2,1)}, bf16[16,4096]{1,0:T(8,128)(2,1)}) fusion(f32[16,4096]{1,0:T(8,128)} %get-tuple-element.4, f32[4096]{0:T(1024)} %convert_element_type.10, f32[16]{0:T(128)S(1)} %rsqrt_reduce_fusion), kind=kLoop, calls=%fused_computation | loop fusion | flops 262144 | bytes 540736 | tf_op jit(solution)/shard_map/convert_element_type | solution.py:344

commit v2 on v1

--- a/solution.py
+++ b/solution.py
@@ -39,9 +39,9 @@
 
 
 def kernel(
-    n_col, n_pair, kp, nt, rt, skew,
+    n_col, n_pair, kp, nt, rt, skew, d_model,
     gate_hbm, up_hbm, w_hbm, res_hbm,
-    out_hbm, sq_out,
+    out_hbm, scale_out,
     gate_v, up_v, hid, w_v, acc, peer, send_buf, recv_buf, own, res_v, total, squares,
     in_sem, w_sem, res_sem, out_sem, ag_send, ag_recv, d_send, d_recv, r_send, r_recv, q_send, q_recv,
 ):
@@ -289,7 +289,7 @@
     whole = squares[0]
     for j in range(1, n_col):
         whole = whole + squares[j]
-    sq_out[...] = whole
+    scale_out[...] = lax.rsqrt(whole / d_model + EPS)
 
 
 def fused_body(n_tp, n_col, kp, nt, rt, width, gate_in, up_in, down_weight, residual, norm_gain):
@@ -300,8 +300,8 @@
     pieces, tiles = depth // kp, local // rt
     any_space = pl.BlockSpec(memory_space=pl.ANY)
     dma = pltpu.SemaphoreType.DMA
-    summed, squares = pl.pallas_call(
-        functools.partial(kernel, n_col, n_pair, kp, nt, rt, min(3, pieces)),
+    summed, scale = pl.pallas_call(
+        functools.partial(kernel, n_col, n_pair, kp, nt, rt, min(3, pieces), width),
         out_shape=(
             jax.ShapeDtypeStruct((own_rows, local), jnp.float32),
             jax.ShapeDtypeStruct((own_rows, 128), jnp.float32),
@@ -339,8 +339,7 @@
         ),
         name="down_reduce",
     )(gate_in, up_in, down_weight, residual)
-    mean_square = squares[:, :1] / width
-    scaled = summed * lax.rsqrt(mean_square + EPS) * norm_gain.astype(jnp.float32)[None, :]
+    scaled = summed * scale[:, :1] * norm_gain.astype(jnp.float32)[None, :]
     return (summed.astype(jnp.bfloat16), scaled.astype(jnp.bfloat16))
 
 

time: 54.2 us -> 54.2 us (level)
  other arithmetic: 3.9 us -> 3.08 us
  local copies, waits for them, and re-layouts: 0 us -> 0.81 us
    rsqrt x1 -> x0, other arithmetic: 0.81 us -> none  [fused_body(): lax.rsqrt(mean_square + EPS)]
    slice x0 -> x1, local copies, waits for them, and re-layouts: none -> 0.81 us  [fused_body(): scaled = summed * scale[:, :1] * norm_gain.astype(jnp.float32)[None, :]]
where the time goes in v2:
time: 54.2 us; the launch traced here: 54 us
  Pallas kernels  49.5 us (91%)
  other arithmetic  3.08 us (6%)
  local copies, waits for them, and re-layouts  0.81 us (1%)
  between operations  0.64 us (1%)
    pallas_call x1, Pallas kernels, fused_body(): pl.pallas_call(functools.partial(kernel, n_col, n_pair, kp, nt, rt, min(3...  49.5 us
    convert_element_type x1, other arithmetic, fused_body(): return (summed.astype(jnp.bfloat16), scaled.astype(jnp.bfloat16))  1.78 us
    convert_element_type x1, other arithmetic, fused_body(): scaled = summed * scale[:, :1] * norm_gain.astype(jnp.float32)[None, :]  1.3 us

profile of v2, /device:TPU:0, one launch (start us, length us, event | category | flops | bytes accessed | tf_op | source)
XLA Modules:
  0.0 54.0 jit_solution(13173097500651015070)
XLA Ops:
  0.6 1.3 %convert_element_type.10 = f32[4096]{0:T(1024)} convert(bf16[4096]{0:T(1024)(128)(2,1)} %param.9) | non-fusion elementwise | flops 4096 | bytes 24576 | tf_op jit(solution)/shard_map/convert_element_type | solution.py:342
  1.9 49.5 %down_reduce.1 = (f32[16,4096]{1,0:T(8,128)}, f32[16,128]{1,0:T(8,128)}) custom-call(bf16[32,6656]{1,0:T(8,128)(2,1)} %gate_hbm.1, bf16[32,6656]{1,0:T(8,128)(2,1)} %up_hbm.1, bf16[6656,4096]{1,0:T(8,128)(2,1)} %w_hbm.1, bf16[16,4096]{1,0:T(8,128)(2,1)} %res_hbm.1), custom_call_target="tpu_custom_call" | custom-call | tf_op jit(solution)/shard_map/down_reduce/pallas_call | solution.py:303
  51.4 0.8 %slice_reduce_fusion = f32[16]{0:T(128)S(1)} fusion(f32[16,128]{1,0:T(8,128)} %get-tuple-element.5), kind=kLoop, calls=%fused_computation.1 | loop fusion | bytes 128 | tf_op jit(solution)/shard_map/slice | solution.py:342
  52.2 1.8 %multiply_convert_fusion = (bf16[16,4096]{1,0:T(8,128)(2,1)}, bf16[16,4096]{1,0:T(8,128)(2,1)}) fusion(f32[16,4096]{1,0:T(8,128)} %get-tuple-element.4, f32[4096]{0:T(1024)} %convert_element_type.10, f32[16]{0:T(128)S(1)} %slice_reduce_fusion), kind=kLoop, calls=%fused_computation | loop fusion | flops 262144 | bytes 540736 | tf_op jit(solution)/shard_map/convert_element_type | solution.py:343
